TPU v7x, 32 devices: a whole 2x2x4 slice. The times are simulated.
32 devices in a mesh: dp: 16 (over z, y, x), tensor: 2 (over core).
Axes of the slice: x: 2, y: 2, z: 4, core: 2. Of those that a mesh axis runs over, the one named last changes fastest.
Arguments:
- gradient: bfloat16 [16, 128, 8192], P('dp', 'tensor'), may hold values from -110 to 110
- momentum: bfloat16 [16, 128, 8192], P('dp', 'tensor'), may hold values from -6 to 6
- indices: int32 [16, 2, 128, 32], P('dp', 'tensor'), may hold values from 0 to 4095, all different within a row
Outputs:
- new_momentum: bfloat16 [16, 128, 8192], P('dp', 'tensor')
- update: bfloat16 [128, 8192], P('tensor')
Inputs may be any that keep to these rules, and one draw needn't show every extreme that they name: The 32 indices of one span of one replica are distinct; index a * 64 + b names row frequency a and column frequency b.
All inputs are finite; a program needn't handle non-finite values.
Results may differ from a plain program's by a relative error of at most 0.0049.
Values may be sent and summed in bfloat16 or wider, within the bound.
A program may use at most 64 MiB of HBM per device.

v0:
```python
import functools

import jax
import jax.numpy as jnp
import numpy as np
from jax import lax
from jax.experimental import pallas as pl
from jax.experimental.pallas import tpu as pltpu
from jax.sharding import PartitionSpec as P

BLOCK = 64
LANES = 128
EPSILON = 1e-06
DECAY = 0.999
F32 = jnp.float32
BF16 = jnp.bfloat16
MESH = pl.DeviceIdType.MESH


def dct_basis(edge):
    frequency = np.arange(edge, dtype=np.float64)[:, None]
    position = np.arange(edge, dtype=np.float64)[None, :]
    waves = np.cos(np.pi * (2.0 * position + 1.0) * frequency / (2.0 * edge))
    weights = np.where(frequency == 0.0, np.sqrt(1.0 / edge), np.sqrt(2.0 / edge))
    return (waves * weights).astype(np.float32)


def halves(x):
    high = x.astype(BF16)
    return high, (x - high.astype(F32)).astype(BF16)


def np_halves(x):
    high = x.astype(jnp.bfloat16)
    return high, (x - high.astype(np.float32)).astype(jnp.bfloat16)


def dot(a, b):
    return jnp.dot(a, b, preferred_element_type=F32)


def dot_nt(a, b):
    return lax.dot_general(a, b, (((1,), (1,)), ((), ())), preferred_element_type=F32)


def wide(x, w_high, w_low):
    rows = x.shape[0]
    high, low = halves(x)
    both = dot(jnp.concatenate([high, low], axis=0), w_high)
    return both[:rows] + both[rows:] + dot(high, w_low)


def kernel(
    replicas, shards, unroll, total,
    grad_ref, mom_ref, idx_ref, fwd_ref, inv_ref, rows_ref, rows3_ref,
    newm_ref, upd_ref,
    by_span, picks, values, factor, ids, all_ids, shipped, all_values,
    span_a, span_b, span_v, dense, e_out, e_in,
    id_sem, value_sem, e_send, e_recv,
):
    me = lax.axis_index("dp")
    part = lax.axis_index("tensor")
    barrier = pltpu.get_barrier_semaphore()

    def greet_dp(k, c):
        pl.semaphore_signal(barrier, inc=1, device_id={"dp": lax.rem(me + k, replicas)}, device_id_type=MESH)
        return c

    def greet_tp(k, c):
        pl.semaphore_signal(barrier, inc=1, device_id={"tensor": lax.rem(part + k, shards)}, device_id_type=MESH)
        return c

    lax.fori_loop(1, replicas, greet_dp, 0)
    lax.fori_loop(1, shards, greet_tp, 0)

    topk, spans = idx_ref.shape
    fold = LANES // topk
    width = fold * BLOCK
    groups = spans // fold

    by_span[...] = idx_ref[...].T
    chosen = jnp.concatenate(
        [by_span[pl.ds(s, groups, stride=fold), :] for s in range(fold)], axis=1
    )
    ids[...] = chosen.astype(jnp.int16)
    picks[0] = (chosen // BLOCK).astype(F32)
    slot = lax.broadcasted_iota(jnp.int32, chosen.shape, 1) // topk
    picks[1] = (chosen % BLOCK + BLOCK * slot).astype(F32)

    zero = jnp.zeros((), BF16)
    one = jnp.ones((), BF16)
    tall = lax.broadcasted_iota(jnp.int32, (width, LANES), 0).astype(F32).astype(BF16)
    short = lax.broadcasted_iota(jnp.int32, (BLOCK, LANES), 0).astype(F32).astype(BF16)

    def hot(levels, plane, g):
        return jnp.where(levels == picks[plane, pl.ds(g, 1), :].astype(BF16), one, zero)

    def columns(g, size):
        return pl.ds(pl.multiple_of(g * size, size), size)

    def renew(g):
        cols = columns(g, width)
        return DECAY * mom_ref[:, cols].astype(F32) + grad_ref[:, cols].astype(F32)

    def encode(step, c):
        batch = [step * unroll + u for u in range(unroll)]
        half_spec = wide(jnp.concatenate([renew(g) for g in batch], axis=0), fwd_ref[0], fwd_ref[1])
        high, low = halves(half_spec)
        found = []
        for u, g in enumerate(batch):
            rows = slice(u * BLOCK, (u + 1) * BLOCK)
            both = dot(jnp.concatenate([high[rows], low[rows]], axis=0), hot(tall, 1, g))
            row_hot = hot(short, 0, g)
            waves = dot(rows_ref[...], jnp.concatenate([row_hot, row_hot], axis=0))
            value = jnp.sum((both[:BLOCK] + both[BLOCK:]) * waves, axis=0, keepdims=True)
            found.append((value, halves(waves * value)))
        for g, (value, pair) in zip(batch, found):
            values[pl.ds(g, 1), :] = value
            factor[:, columns(g, 2 * LANES)] = jnp.concatenate(pair, axis=1)
        return c

    def restore(step, c):
        batch = [step * unroll + u for u in range(unroll)]
        spread = []
        for g in batch:
            col_hot = hot(tall, 1, g)
            spread.append(dot_nt(factor[:, columns(g, 2 * LANES)], jnp.concatenate([col_hot, col_hot], axis=1)))
        restored = wide(jnp.concatenate(spread, axis=0), inv_ref[0], inv_ref[1])
        for u, g in enumerate(batch):
            newm_ref[:, columns(g, width)] = (renew(g) - restored[u * BLOCK:(u + 1) * BLOCK]).astype(BF16)
        return c

    def copy_dp(src, dst, sems, k, slot):
        return pltpu.make_async_remote_copy(
            src_ref=src, dst_ref=dst.at[slot],
            send_sem=sems.at[0, k], recv_sem=sems.at[1, k],
            device_id={"dp": lax.rem(me + k, replicas)}, device_id_type=MESH,
        )

    def to_all(src, dst, sems):
        def start(k, c):
            copy_dp(src, dst, sems, k, me).start()
            return c
        lax.fori_loop(1, replicas, start, 0)
        dst[me] = src[...]

    def from_all(src, dst, sems):
        def finish(k, c):
            copy_dp(src, dst, sems, k, lax.rem(me - k + replicas, replicas)).wait_recv()
            return c
        lax.fori_loop(1, replicas, finish, 0)

    def sent_all(src, dst, sems):
        def finish(k, c):
            copy_dp(src, dst, sems, k, me).wait_send()
            return c
        lax.fori_loop(1, replicas, finish, 0)

    steps = groups // unroll
    lax.fori_loop(0, steps // 2, encode, 0)
    pl.semaphore_wait(barrier, replicas - 1 + shards - 1)
    to_all(ids, all_ids, id_sem)
    lax.fori_loop(steps // 2, steps, encode, 0)
    shipped[...] = values[...].astype(BF16)
    to_all(shipped, all_values, value_sem)
    lax.fori_loop(0, steps, restore, 0)
    from_all(ids, all_ids, id_sem)
    from_all(shipped, all_values, value_sem)

    for s in range(fold):
        lines = slice(s * groups, (s + 1) * groups)
        lanes = slice(s * topk, (s + 1) * topk)
        span_v[lines, :] = jnp.concatenate([all_values[r].astype(F32)[:, lanes] for r in range(replicas)], axis=1)
        named = jnp.concatenate([all_ids[r].astype(jnp.int32)[:, lanes] for r in range(replicas)], axis=1)
        span_a[lines, :] = (named // BLOCK).astype(F32)
        span_b[lines, :] = (named % BLOCK).astype(F32)

    depth = replicas * topk
    level = lax.broadcasted_iota(jnp.int32, (BLOCK, depth), 0).astype(F32).astype(BF16)

    def densify(step, energy):
        tiles = []
        for s in range(fold):
            lines = pl.ds(pl.multiple_of(s * groups + step * 8, 8), 8)
            tiles.append([ref[lines, :] for ref in (span_a, span_b, span_v)])
        for u in range(8):
            blocks = []
            for s in range(fold):
                a, b, v = (tile[u:u + 1].astype(BF16) for tile in tiles[s])
                row_hot = jnp.where(level == a, v, zero)
                col_hot = jnp.where(level == b, one, zero)
                blocks.append(dot_nt(row_hot, col_hot))
            combined = jnp.concatenate(blocks, axis=1)
            dense[:, columns(step * 8 + u, width)] = combined
            energy = energy + jnp.sum((combined * combined).reshape(BLOCK // 8, 8, width), axis=0)
        return energy

    energy = lax.fori_loop(0, groups // 8, densify, jnp.zeros((8, width), F32))
    energy = sum(energy[:, n * LANES:(n + 1) * LANES] for n in range(width // LANES))
    e_out[...] = energy
    e_in[part] = energy

    def copy_tp(k, slot):
        return pltpu.make_async_remote_copy(
            src_ref=e_out, dst_ref=e_in.at[slot],
            send_sem=e_send.at[k], recv_sem=e_recv.at[k],
            device_id={"tensor": lax.rem(part + k, shards)}, device_id_type=MESH,
        )

    def start_tp(k, c):
        copy_tp(k, part).start()
        return c

    lax.fori_loop(1, shards, start_tp, 0)

    def decode(step, c):
        batch = [columns(step * unroll + u, width) for u in range(unroll)]
        across = wide(jnp.concatenate([dense[:, cols] for cols in batch], axis=0), inv_ref[0], inv_ref[1])
        high, low = halves(across)
        done = []
        for u in range(unroll):
            rows = slice(u * BLOCK, (u + 1) * BLOCK)
            done.append(dot(rows3_ref[...], jnp.concatenate([high[rows], high[rows], low[rows]], axis=0)))
        for cols, block in zip(batch, done):
            dense[:, cols] = block
        return c

    lax.fori_loop(0, groups // unroll, decode, 0)

    def finish_tp(k, c):
        copy_tp(k, lax.rem(part - k + shards, shards)).wait()
        return c

    lax.fori_loop(1, shards, finish_tp, 0)
    mean = jnp.sum(e_in[...]) / total
    scale = lax.rsqrt(jnp.full((1, width), mean + EPSILON, F32))

    def finish(step, c):
        for u in range(unroll):
            cols = columns(step * unroll + u, width)
            upd_ref[:, cols] = (dense[:, cols] * scale).astype(BF16)
        return c

    lax.fori_loop(0, groups // unroll, finish, 0)
    sent_all(ids, all_ids, id_sem)
    sent_all(shipped, all_values, value_sem)


def local(gradient, momentum, indices, replicas, shards):
    height, cols = gradient.shape[1:]
    topk = indices.shape[-1]
    fold = LANES // topk
    spans = cols // BLOCK
    groups = spans // fold
    assert height == BLOCK and groups * fold == spans
    basis = dct_basis(BLOCK)
    eye = np.eye(fold, dtype=np.float32)
    fwd = jnp.asarray(np.stack(np_halves(np.kron(eye, basis.T))))
    inv = jnp.asarray(np.stack(np_halves(np.kron(eye, basis))))
    high, low = np_halves(basis.T)
    rows = jnp.asarray(np.concatenate([high, low], axis=1))
    rows3 = jnp.asarray(np.concatenate([high, low, high], axis=1))
    depth = max(replicas * topk, LANES)
    vmem = pl.BlockSpec(memory_space=pltpu.VMEM)
    newm, update = pl.pallas_call(
        functools.partial(kernel, replicas, shards, 8, float(height * cols * shards)),
        out_shape=(
            jax.ShapeDtypeStruct((height, cols), BF16),
            jax.ShapeDtypeStruct((height, cols), BF16),
        ),
        in_specs=[vmem] * 7,
        out_specs=(vmem, vmem),
        scratch_shapes=[
            pltpu.VMEM((spans, topk), jnp.int32),
            pltpu.VMEM((2, groups, LANES), F32),
            pltpu.VMEM((groups, LANES), F32),
            pltpu.VMEM((height, groups * 2 * LANES), BF16),
            pltpu.VMEM((groups, LANES), jnp.int16),
            pltpu.VMEM((replicas, groups, LANES), jnp.int16),
            pltpu.VMEM((groups, LANES), BF16),
            pltpu.VMEM((replicas, groups, LANES), BF16),
            pltpu.VMEM((spans, depth), F32),
            pltpu.VMEM((spans, depth), F32),
            pltpu.VMEM((spans, depth), F32),
            pltpu.VMEM((height, cols), F32),
            pltpu.VMEM((8, LANES), F32),
            pltpu.VMEM((shards, 8, LANES), F32),
            pltpu.SemaphoreType.DMA((2, replicas)),
            pltpu.SemaphoreType.DMA((2, replicas)),
            pltpu.SemaphoreType.DMA((shards,)),
            pltpu.SemaphoreType.DMA((shards,)),
        ],
        compiler_params=pltpu.CompilerParams(collective_id=0, has_side_effects=True),
        name="demo_step",
    )(gradient[0], momentum[0], indices.reshape(spans, topk).T, fwd, inv, rows, rows3)
    return newm[None], update


def solution(mesh):
    in_specs = (P("dp", "tensor", None), P("dp", "tensor", None), P("dp", "tensor", None, None))
    out_specs = (P("dp", "tensor", None), P("tensor", None))
    body = functools.partial(local, replicas=mesh.shape["dp"], shards=mesh.shape["tensor"])
    return jax.shard_map(body, mesh=mesh, in_specs=in_specs, out_specs=out_specs, check_vma=False)
```

profile of v0, /device:TPU:0, one launch (start us, length us, event | category | flops | bytes accessed | tf_op | source)
XLA Modules:
  0.0 28.1 jit_solution(4556157818871999355)
XLA Ops:
  0.6 24.1 %demo_step.1 = (bf16[64,8192]{1,0:T(8,128)(2,1)}, bf16[64,8192]{1,0:T(8,128)(2,1)}) custom-call(bf16[64,8192]{1,0:T(8,128)(2,1)} %bitcast.7, bf16[64,8192]{1,0:T(8,128)(2,1)} %bitcast.8, s32[32,128]{1,0:T(8,128)} %bitcast.9, bf16[2,256,256]{2,1,0:T(8,128)(2,1)} %constant.8.clone.fwd_ref, bf16[2,256,256]{2,1,0:T(8,128)(2,1)} %constant.9.clone.inv_ref, ...), custom_call_target="tpu_custom_call" | custom-call | tf_op jit(solution)/shard_map/demo_step/pallas_call | solution.py:265
  24.8 0.0 copy-start
  24.8 2.4 %copy.11 = bf16[1,64,8192]{2,1,0:T(8,128)(2,1)} copy(bf16[1,64,8192]{2,1,0:T(8,128)(2,1)} %bitcast.6) | data formatting | bytes 2097152
  27.1 0.0 copy-done
  27.1 1.0 %copy.12 = bf16[64,8192]{1,0:T(8,128)(2,1)} copy(bf16[64,8192]{1,0:T(8,128)(2,1)S(1)} %copy-done) | data formatting | bytes 2097152
Async XLA Ops:
  24.8 2.4 %copy-start = (bf16[64,8192]{1,0:T(8,128)(2,1)S(1)}, bf16[64,8192]{1,0:T(8,128)(2,1)}, u32[]{:S(2)}) copy-start(bf16[64,8192]{1,0:T(8,128)(2,1)} %get-tuple-element.9) | copy-start | bytes 3145732
where the time goes:
time: 28.3 us; the launch traced here: 28.1 us
  Pallas kernels  24.1 us (85%)
  local copies, waits for them, and re-layouts  3.32 us (12%)
  between operations  0.65 us (2%)
    pallas_call x1, Pallas kernels, local(): pl.pallas_call(functools.partial(kernel, replicas, shards, 8, float(heigh...  24.1 us
    unnamed x4, local copies, waits for them, and re-layouts  3.32 us

commit v1 on v0

v1 whole, which is shorter than its diff:
```python
import functools

import jax
import jax.numpy as jnp
import numpy as np
from jax import lax
from jax.experimental import pallas as pl
from jax.experimental.pallas import tpu as pltpu
from jax.sharding import PartitionSpec as P

BLOCK = 64
LANES = 128
SUBLANES = 8
EPSILON = 1e-06
DECAY = 0.999
F32 = jnp.float32
BF16 = jnp.bfloat16
MESH = pl.DeviceIdType.MESH


def dct_basis(edge):
    frequency = np.arange(edge, dtype=np.float64)[:, None]
    position = np.arange(edge, dtype=np.float64)[None, :]
    waves = np.cos(np.pi * (2.0 * position + 1.0) * frequency / (2.0 * edge))
    weights = np.where(frequency == 0.0, np.sqrt(1.0 / edge), np.sqrt(2.0 / edge))
    return (waves * weights).astype(np.float32)


def halves(x):
    high = x.astype(BF16)
    return high, (x - high.astype(F32)).astype(BF16)


def np_halves(x):
    high = x.astype(jnp.bfloat16)
    return high, (x - high.astype(np.float32)).astype(jnp.bfloat16)


def dot(a, b):
    return jnp.dot(a, b, preferred_element_type=F32)


def dot_nt(a, b):
    return lax.dot_general(a, b, (((1,), (1,)), ((), ())), preferred_element_type=F32)


def wide(blocks, weights):
    tiles = [block[:, n * LANES:(n + 1) * LANES] for block in blocks for n in range(2)]
    high, low = halves(jnp.concatenate(tiles, axis=0))
    both = dot(jnp.concatenate([high, low], axis=1), weights)
    out = both[:, :LANES] + both[:, LANES:]
    parts = [out[n * BLOCK:(n + 1) * BLOCK] for n in range(len(tiles))]
    return [jnp.concatenate(parts[2 * n:2 * n + 2], axis=1) for n in range(len(blocks))]


def kernel(
    replicas, shards,
    grad_hbm, mom_hbm, idx_hbm, fwd_hbm, inv_hbm, deep_hbm, rows_hbm,
    newm_ref, dense_ref, e_in,
    grad, mom, idx, fwd, inv, deep, rows,
    by_span, picks, high_even, low_even, high_odd, low_odd, factor,
    ids, all_ids, shipped, all_values, span_a, span_b, span_v, mixed_even, mixed_odd, e_out,
    x_sem, c_sem, id_sem, value_sem, e_send, e_recv,
):
    me = lax.axis_index("dp")
    part = lax.axis_index("tensor")
    barrier = pltpu.get_barrier_semaphore()

    topk, spans = idx.shape
    fold = LANES // topk
    width = fold * BLOCK
    groups = spans // fold
    chunks = groups // SUBLANES
    stretch = SUBLANES * width
    depth = replicas * topk

    loads = [pltpu.make_async_copy(src, dst, c_sem.at[n]) for n, (src, dst) in enumerate(
        [(idx_hbm, idx), (fwd_hbm, fwd), (rows_hbm, rows), (inv_hbm, inv), (deep_hbm, deep)])]

    def slab(c):
        cols = pl.ds(c * stretch, stretch)
        return [pltpu.make_async_copy(src.at[:, cols], dst.at[:, cols], x_sem.at[n, c])
                for n, (src, dst) in enumerate([(mom_hbm, mom), (grad_hbm, grad)])]

    loads[0].start()
    loads[1].start()
    for copy in slab(0):
        copy.start()
    loads[2].start()
    for c in range(1, chunks):
        for copy in slab(c):
            copy.start()
    loads[3].start()
    loads[4].start()

    def greet_dp(k, c):
        pl.semaphore_signal(barrier, inc=1, device_id={"dp": lax.rem(me + k, replicas)}, device_id_type=MESH)
        return c

    def greet_tp(k, c):
        pl.semaphore_signal(barrier, inc=1, device_id={"tensor": lax.rem(part + k, shards)}, device_id_type=MESH)
        return c

    lax.fori_loop(1, replicas, greet_dp, 0)
    lax.fori_loop(1, shards, greet_tp, 0)

    loads[0].wait()
    by_span[...] = idx[...].T
    chosen = jnp.concatenate(
        [by_span[pl.ds(s, groups, stride=fold), :] for s in range(fold)], axis=1
    )
    ids[...] = chosen.astype(jnp.int16)
    picks[0] = (chosen // BLOCK).astype(F32)
    slot = lax.broadcasted_iota(jnp.int32, chosen.shape, 1) // topk
    picks[1] = (chosen % BLOCK + BLOCK * slot).astype(F32)

    zero = jnp.zeros((), BF16)
    one = jnp.ones((), BF16)
    tall = lax.broadcasted_iota(jnp.int32, (width, LANES), 0).astype(F32).astype(BF16)
    short = lax.broadcasted_iota(jnp.int32, (BLOCK, LANES), 0).astype(F32).astype(BF16)
    level = lax.broadcasted_iota(jnp.int32, (BLOCK, depth), 0).astype(F32).astype(BF16)

    def hot(levels, plane, g):
        return jnp.where(levels == picks[plane, pl.ds(g, 1), :].astype(BF16), one, zero)

    def columns(g, size):
        return pl.ds(g * size, size)

    def members(c):
        return range(c * SUBLANES, (c + 1) * SUBLANES)

    def renew(g):
        cols = columns(g, width)
        return DECAY * mom[:, cols].astype(F32) + grad[:, cols].astype(F32)

    highs, lows = (high_even, high_odd), (low_even, low_odd)

    def transform(c):
        high, low = highs[c % 2], lows[c % 2]
        for u, block in enumerate(wide([renew(g) for g in members(c)], fwd[...])):
            high[u], low[u] = halves(block)

    def pick(c):
        high, low = highs[c % 2], lows[c % 2]
        found = []
        for u, g in enumerate(members(c)):
            both = dot(jnp.concatenate([high[u], low[u]], axis=0), hot(tall, 1, g))
            row_hot = hot(short, 0, g)
            waves = dot(rows[...], jnp.concatenate([row_hot, row_hot], axis=0))
            value = jnp.sum((both[:BLOCK] + both[BLOCK:]) * waves, axis=0, keepdims=True)
            found.append(value)
            factor[:, columns(g, 2 * LANES)] = jnp.concatenate(halves(waves * value), axis=1)
        shipped[c] = jnp.concatenate(found, axis=0).astype(BF16)

    def restore(c):
        spread = []
        for g in members(c):
            col_hot = hot(tall, 1, g)
            spread.append(dot_nt(factor[:, columns(g, 2 * LANES)], jnp.concatenate([col_hot, col_hot], axis=1)))
        for g, block in zip(members(c), wide(spread, inv[...])):
            newm_ref[:, columns(g, width)] = (renew(g) - block).astype(BF16)

    def id_copy(k, slot):
        return pltpu.make_async_remote_copy(
            src_ref=ids, dst_ref=all_ids.at[slot],
            send_sem=id_sem.at[0, k], recv_sem=id_sem.at[1, k],
            device_id={"dp": lax.rem(me + k, replicas)}, device_id_type=MESH,
        )

    def value_copy(c, k, slot):
        return pltpu.make_async_remote_copy(
            src_ref=shipped.at[c], dst_ref=all_values.at[c, slot],
            send_sem=value_sem.at[c, 0, k], recv_sem=value_sem.at[c, 1, k],
            device_id={"dp": lax.rem(me + k, replicas)}, device_id_type=MESH,
        )

    def each(act):
        def step(k, c):
            act(k)
            return c
        lax.fori_loop(1, replicas, step, 0)

    def source(k):
        return lax.rem(me - k + replicas, replicas)

    def ship(c):
        each(lambda k: value_copy(c, k, me).start())
        all_values[c, me] = shipped[c]

    loads[1].wait()
    for copy in slab(0):
        copy.wait()
    transform(0)
    loads[2].wait()
    for c in range(chunks):
        if c + 1 < chunks:
            for copy in slab(c + 1):
                copy.wait()
            transform(c + 1)
        pick(c)
        if c == 0:
            pl.semaphore_wait(barrier, replicas - 1 + shards - 1)
            each(lambda k: id_copy(k, me).start())
            all_ids[me] = ids[...]
        ship(c)

    loads[3].wait()
    loads[4].wait()
    for c in range(chunks):
        restore(c)

    each(lambda k: id_copy(k, source(k)).wait_recv())
    for s in range(fold):
        lines = slice(s * groups, (s + 1) * groups)
        lanes = slice(s * topk, (s + 1) * topk)
        named = jnp.concatenate([all_ids[r].astype(jnp.int32)[:, lanes] for r in range(replicas)], axis=1)
        span_a[lines, :] = (named // BLOCK).astype(F32)
        span_b[lines, :] = (named % BLOCK).astype(F32)

    mixes = (mixed_even, mixed_odd)

    def densify(c, energy):
        mixed = mixes[c % 2]
        tiles = []
        for s in range(fold):
            lanes = slice(s * topk, (s + 1) * topk)
            lines = pl.ds(s * groups + c * SUBLANES, SUBLANES)
            span_v[s] = jnp.concatenate([all_values[c, r].astype(F32)[:, lanes] for r in range(replicas)], axis=1)
            tiles.append((span_a[lines, :], span_b[lines, :], span_v[s]))
        for u in range(SUBLANES):
            blocks = []
            for s in range(fold):
                a, b, v = (tile[u:u + 1].astype(BF16) for tile in tiles[s])
                row_hot = jnp.where(level == a, v, zero)
                col_hot = jnp.where(level == b, one, zero)
                blocks.append(dot_nt(row_hot, col_hot))
            combined = jnp.concatenate(blocks, axis=1)
            mixed[u] = combined.astype(BF16)
            energy = energy + jnp.sum((combined * combined).reshape(BLOCK // SUBLANES, SUBLANES, width), axis=0)
        return energy

    def decode(c):
        mixed = mixes[c % 2]
        tall_mix = jnp.concatenate([mixed[u] for u in range(SUBLANES)], axis=0)
        across = dot(jnp.concatenate([tall_mix, tall_mix], axis=1), deep[...]).astype(BF16)
        for u, g in enumerate(members(c)):
            block = across[u * BLOCK:(u + 1) * BLOCK]
            dense_ref[:, columns(g, width)] = dot(rows[...], jnp.concatenate([block, block], axis=0))

    energy = jnp.zeros((SUBLANES, width), F32)
    for c in range(chunks):
        each(lambda k: value_copy(c, k, source(k)).wait_recv())
        energy = densify(c, energy)
        if c:
            decode(c - 1)

    energy = sum(energy[:, n * LANES:(n + 1) * LANES] for n in range(width // LANES))
    e_out[...] = energy
    e_in[part] = energy

    def copy_tp(k, slot):
        return pltpu.make_async_remote_copy(
            src_ref=e_out, dst_ref=e_in.at[slot],
            send_sem=e_send.at[k], recv_sem=e_recv.at[k],
            device_id={"tensor": lax.rem(part + k, shards)}, device_id_type=MESH,
        )

    def start_tp(k, c):
        copy_tp(k, part).start()
        return c

    def finish_tp(k, c):
        copy_tp(k, lax.rem(part - k + shards, shards)).wait()
        return c

    lax.fori_loop(1, shards, start_tp, 0)
    decode(chunks - 1)
    each(lambda k: id_copy(k, me).wait_send())
    for c in range(chunks):
        each(lambda k: value_copy(c, k, me).wait_send())
    lax.fori_loop(1, shards, finish_tp, 0)


def finish(total, newm_ref, dense_ref, e_ref, newm_hbm, upd_hbm, upd, sems):
    first = pltpu.make_async_copy(newm_ref, newm_hbm, sems.at[0])
    first.start()
    pieces = sems.shape[0] - 1
    stretch = upd.shape[1] // pieces
    mean = jnp.sum(e_ref[...]) / total
    scale = lax.rsqrt(jnp.full((1, stretch), mean + EPSILON, F32))
    copies = []
    for n in range(pieces):
        cols = pl.ds(n * stretch, stretch)
        upd[:, cols] = (dense_ref[:, cols] * scale).astype(BF16)
        copies.append(pltpu.make_async_copy(upd.at[:, cols], upd_hbm.at[:, cols], sems.at[n + 1]))
        copies[-1].start()
    first.wait()
    for copy in copies:
        copy.wait()


def local(gradient, momentum, indices, replicas, shards):
    height, cols = gradient.shape[1:]
    topk = indices.shape[-1]
    fold = LANES // topk
    spans = cols // BLOCK
    groups = spans // fold
    width = fold * BLOCK
    chunks = groups // SUBLANES
    assert height == BLOCK and chunks * SUBLANES * fold == spans and width == 2 * LANES
    basis = dct_basis(BLOCK)
    pair = np.eye(2, dtype=np.float32)
    both = [np.concatenate(np_halves(np.kron(pair, w)), axis=1) for w in (basis.T, basis)]
    fwd, inv = (jnp.asarray(np.concatenate([w, w], axis=0)) for w in both)
    deep = jnp.asarray(np.concatenate(np_halves(np.kron(np.eye(fold, dtype=np.float32), basis)), axis=0))
    rows = jnp.asarray(np.concatenate(np_halves(basis.T), axis=1))
    depth = max(replicas * topk, LANES)
    vmem = pl.BlockSpec(memory_space=pltpu.VMEM)
    hbm = pl.BlockSpec(memory_space=pltpu.HBM)
    half = pltpu.VMEM((SUBLANES, height, width), BF16)
    operands = (gradient[0], momentum[0], indices.reshape(spans, topk).T, fwd, inv, deep, rows)
    newm, dense, energy = pl.pallas_call(
        functools.partial(kernel, replicas, shards),
        out_shape=(
            jax.ShapeDtypeStruct((height, cols), BF16),
            jax.ShapeDtypeStruct((height, cols), F32),
            jax.ShapeDtypeStruct((shards, SUBLANES, LANES), F32),
        ),
        in_specs=[hbm] * 7,
        out_specs=(vmem, vmem, vmem),
        scratch_shapes=[
            pltpu.VMEM((height, cols), BF16),
            pltpu.VMEM((height, cols), BF16),
            pltpu.VMEM((topk, spans), jnp.int32),
            pltpu.VMEM(fwd.shape, BF16),
            pltpu.VMEM(inv.shape, BF16),
            pltpu.VMEM(deep.shape, BF16),
            pltpu.VMEM(rows.shape, BF16),
            pltpu.VMEM((spans, topk), jnp.int32),
            pltpu.VMEM((2, groups, LANES), F32),
            half, half, half, half,
            pltpu.VMEM((height, groups * 2 * LANES), BF16),
            pltpu.VMEM((groups, LANES), jnp.int16),
            pltpu.VMEM((replicas, groups, LANES), jnp.int16),
            pltpu.VMEM((chunks, SUBLANES, LANES), BF16),
            pltpu.VMEM((chunks, replicas, SUBLANES, LANES), BF16),
            pltpu.VMEM((spans, depth), F32),
            pltpu.VMEM((spans, depth), F32),
            pltpu.VMEM((fold, SUBLANES, depth), F32),
            half, half,
            pltpu.VMEM((SUBLANES, LANES), F32),
            pltpu.SemaphoreType.DMA((2, chunks)),
            pltpu.SemaphoreType.DMA((5,)),
            pltpu.SemaphoreType.DMA((2, replicas)),
            pltpu.SemaphoreType.DMA((chunks, 2, replicas)),
            pltpu.SemaphoreType.DMA((shards,)),
            pltpu.SemaphoreType.DMA((shards,)),
        ],
        compiler_params=pltpu.CompilerParams(
            collective_id=0, has_side_effects=True, vmem_limit_bytes=24 * 2 ** 20
        ),
        name="demo_step",
    )(*(pltpu.with_memory_space_constraint(x, pltpu.HBM) for x in operands))
    newm, update = pl.pallas_call(
        functools.partial(finish, float(height * cols * shards)),
        out_shape=(
            jax.ShapeDtypeStruct((height, cols), BF16),
            jax.ShapeDtypeStruct((height, cols), BF16),
        ),
        in_specs=[vmem] * 3,
        out_specs=(hbm, hbm),
        scratch_shapes=[pltpu.VMEM((height, cols), BF16), pltpu.SemaphoreType.DMA((5,))],
        compiler_params=pltpu.CompilerParams(vmem_limit_bytes=8 * 2 ** 20),
        name="finish",
    )(newm, dense, energy)
    return newm[None], update


def solution(mesh):
    in_specs = (P("dp", "tensor", None), P("dp", "tensor", None), P("dp", "tensor", None, None))
    out_specs = (P("dp", "tensor", None), P("tensor", None))
    body = functools.partial(local, replicas=mesh.shape["dp"], shards=mesh.shape["tensor"])
    return jax.shard_map(body, mesh=mesh, in_specs=in_specs, out_specs=out_specs, check_vma=False)
```

time: 28.3 us -> 23.2 us (0.82)
  local copies, waits for them, and re-layouts: 3.32 us -> 0 us
  Pallas kernels: 24.1 us -> 22.4 us
    unnamed x4 -> x0, local copies, waits for them, and re-layouts: 3.32 us -> none
    pallas_call x1 -> x2, Pallas kernels: 24.1 us -> 22.4 us  [the longest x1 21.1 us: local(): pl.pallas_call(functools.partial(kernel, replicas, shards), out_shape=(ja...]
where the time goes in v1:
time: 23.2 us; the launch traced here: 23.1 us
  Pallas kernels  22.4 us (97%)
  between operations  0.64 us (3%)
    pallas_call x1, Pallas kernels, local(): pl.pallas_call(functools.partial(kernel, replicas, shards), out_shape=(ja...  21.1 us
    pallas_call x1, Pallas kernels, local(): pl.pallas_call(functools.partial(finish, float(height * cols * shards)),...  1.35 us

profile of v1, /device:TPU:0, one launch (start us, length us, event | category | flops | bytes accessed | tf_op | source)
XLA Modules:
  0.0 23.1 jit_solution(15120271618100991477)
XLA Ops:
  0.6 21.1 %demo_step.1 = (bf16[64,8192]{1,0:T(8,128)(2,1)S(1)}, f32[64,8192]{1,0:T(8,128)S(1)}, f32[2,8,128]{2,1,0:T(8,128)S(1)}) custom-call(bf16[64,8192]{1,0:T(8,128)(2,1)} %bitcast.6, bf16[64,8192]{1,0:T(8,128)(2,1)} %bitcast.7, s32[32,128]{1,0:T(8,128)} %bitcast.8, bf16[256,256]{1,0:T(8,128)(2,1)} %constant.8.clone.fwd_hbm, ...), custom_call_target="tpu_custom_call" | custom-call | tf_op jit(solution)/shard_map/demo_step/pallas_call | solution.py:322
  21.7 1.4 %finish.1 = (bf16[64,8192]{1,0:T(8,128)(2,1)}, bf16[64,8192]{1,0:T(8,128)(2,1)}) custom-call(bf16[64,8192]{1,0:T(8,128)(2,1)S(1)} %get-tuple-element.7.newm_ref, f32[64,8192]{1,0:T(8,128)S(1)} %get-tuple-element.8.dense_ref, f32[2,8,128]{2,1,0:T(8,128)S(1)} %get-tuple-element.9.e_ref), custom_call_target="tpu_custom_call" | custom-call | tf_op jit(solution)/shard_map/finish/pallas_call | solution.py:364

commit v2 on v1

--- a/solution.py
+++ b/solution.py
@@ -59,8 +59,8 @@
     newm_ref, dense_ref, e_in,
     grad, mom, idx, fwd, inv, deep, rows,
     by_span, picks, high_even, low_even, high_odd, low_odd, factor,
-    ids, all_ids, shipped, all_values, span_a, span_b, span_v, mixed_even, mixed_odd, e_out,
-    x_sem, c_sem, id_sem, value_sem, e_send, e_recv,
+    ids, all_ids, values, shipped, all_values, span_a, span_b, span_v, partial, mixed, e_out,
+    x_sem, c_sem, id_sem, value_sem, id_in, value_in, ready, e_send, e_recv,
 ):
     me = lax.axis_index("dp")
     part = lax.axis_index("tensor")
@@ -72,7 +72,10 @@
     groups = spans // fold
     chunks = groups // SUBLANES
     stretch = SUBLANES * width
-    depth = replicas * topk
+    team = all_ids.shape[1]
+    teams = replicas // team
+    depth = team * topk
+    home = me // team
 
     loads = [pltpu.make_async_copy(src, dst, c_sem.at[n]) for n, (src, dst) in enumerate(
         [(idx_hbm, idx), (fwd_hbm, fwd), (rows_hbm, rows), (inv_hbm, inv), (deep_hbm, deep)])]
@@ -93,16 +96,22 @@
     loads[3].start()
     loads[4].start()
 
-    def greet_dp(k, c):
-        pl.semaphore_signal(barrier, inc=1, device_id={"dp": lax.rem(me + k, replicas)}, device_id_type=MESH)
-        return c
-
-    def greet_tp(k, c):
-        pl.semaphore_signal(barrier, inc=1, device_id={"tensor": lax.rem(part + k, shards)}, device_id_type=MESH)
-        return c
-
-    lax.fori_loop(1, replicas, greet_dp, 0)
-    lax.fori_loop(1, shards, greet_tp, 0)
+    def each(low, high, act):
+        def step(k, c):
+            act(k)
+            return c
+        lax.fori_loop(low, high, step, 0)
+
+    def peer(j):
+        return dict(device_id={"dp": j}, device_id_type=MESH)
+
+    def mate(k):
+        return dict(device_id={"tensor": lax.rem(part + k, shards)}, device_id_type=MESH)
+
+    each(me + 1, replicas, lambda j: pl.semaphore_signal(barrier, inc=1, **peer(j)))
+    each(1, shards, lambda k: pl.semaphore_signal(barrier, inc=1, **mate(k)))
+    pl.semaphore_wait(barrier, me + shards - 1)
+    each(0, me, lambda j: pl.semaphore_signal(ready.at[me], inc=1, **peer(j)))
 
     loads[0].wait()
     by_span[...] = idx[...].T
@@ -142,15 +151,13 @@
 
     def pick(c):
         high, low = highs[c % 2], lows[c % 2]
-        found = []
         for u, g in enumerate(members(c)):
             both = dot(jnp.concatenate([high[u], low[u]], axis=0), hot(tall, 1, g))
             row_hot = hot(short, 0, g)
             waves = dot(rows[...], jnp.concatenate([row_hot, row_hot], axis=0))
             value = jnp.sum((both[:BLOCK] + both[BLOCK:]) * waves, axis=0, keepdims=True)
-            found.append(value)
+            values[pl.ds(g, 1), :] = value
             factor[:, columns(g, 2 * LANES)] = jnp.concatenate(halves(waves * value), axis=1)
-        shipped[c] = jnp.concatenate(found, axis=0).astype(BF16)
 
     def restore(c):
         spread = []
@@ -160,32 +167,31 @@
         for g, block in zip(members(c), wide(spread, inv[...])):
             newm_ref[:, columns(g, width)] = (renew(g) - block).astype(BF16)
 
-    def id_copy(k, slot):
+    def copies(src, dst, sends, arrivals, j):
         return pltpu.make_async_remote_copy(
-            src_ref=ids, dst_ref=all_ids.at[slot],
-            send_sem=id_sem.at[0, k], recv_sem=id_sem.at[1, k],
-            device_id={"dp": lax.rem(me + k, replicas)}, device_id_type=MESH,
+            src_ref=src, dst_ref=dst.at[home, lax.rem(me, team)],
+            send_sem=sends.at[0], recv_sem=arrivals.at[home], **peer(j),
         )
 
-    def value_copy(c, k, slot):
+    def send_ids(j):
+        copies(ids, all_ids, id_sem, id_in, j).start()
+
+    def send_values(j):
+        copies(shipped, all_values, value_sem, value_in, j).start()
+
+    def greet(j):
+        pl.semaphore_wait(ready.at[j], 1)
+        send_ids(j)
+        send_values(j)
+
+    def bulk(dst, sends, arrivals, t, count):
+        ref = dst.at[t, pl.ds(0, count)]
         return pltpu.make_async_remote_copy(
-            src_ref=shipped.at[c], dst_ref=all_values.at[c, slot],
-            send_sem=value_sem.at[c, 0, k], recv_sem=value_sem.at[c, 1, k],
-            device_id={"dp": lax.rem(me + k, replicas)}, device_id_type=MESH,
+            src_ref=ref, dst_ref=ref, send_sem=sends.at[0], recv_sem=arrivals.at[t], **peer(me),
         )
 
-    def each(act):
-        def step(k, c):
-            act(k)
-            return c
-        lax.fori_loop(1, replicas, step, 0)
-
-    def source(k):
-        return lax.rem(me - k + replicas, replicas)
-
-    def ship(c):
-        each(lambda k: value_copy(c, k, me).start())
-        all_values[c, me] = shipped[c]
+    each(0, me, send_ids)
+    all_ids[home, lax.rem(me, team)] = ids[...]
 
     loads[1].wait()
     for copy in slab(0):
@@ -198,61 +204,72 @@
                 copy.wait()
             transform(c + 1)
         pick(c)
-        if c == 0:
-            pl.semaphore_wait(barrier, replicas - 1 + shards - 1)
-            each(lambda k: id_copy(k, me).start())
-            all_ids[me] = ids[...]
-        ship(c)
+    shipped[...] = values[...].astype(BF16)
+    each(0, me, send_values)
+    all_values[home, lax.rem(me, team)] = shipped[...]
 
     loads[3].wait()
+    restore(0)
+    each(me + 1, (home + 1) * team, greet)
+    for c in range(1, chunks):
+        restore(c)
+    each((home + 1) * team, replicas, greet)
     loads[4].wait()
-    for c in range(chunks):
-        restore(c)
-
-    each(lambda k: id_copy(k, source(k)).wait_recv())
-    for s in range(fold):
-        lines = slice(s * groups, (s + 1) * groups)
-        lanes = slice(s * topk, (s + 1) * topk)
-        named = jnp.concatenate([all_ids[r].astype(jnp.int32)[:, lanes] for r in range(replicas)], axis=1)
-        span_a[lines, :] = (named // BLOCK).astype(F32)
-        span_b[lines, :] = (named % BLOCK).astype(F32)
-
-    mixes = (mixed_even, mixed_odd)
-
-    def densify(c, energy):
-        mixed = mixes[c % 2]
+
+    def name(n, t):
+        for s in range(fold):
+            lines = slice(s * groups, (s + 1) * groups)
+            lanes = slice(s * topk, (s + 1) * topk)
+            named = jnp.concatenate([all_ids[t, r].astype(jnp.int32)[:, lanes] for r in range(team)], axis=1)
+            span_a[n, lines, :] = (named // BLOCK).astype(F32)
+            span_b[n, lines, :] = (named % BLOCK).astype(F32)
+
+    def gather(n, t):
+        for s in range(fold):
+            lines = slice(s * groups, (s + 1) * groups)
+            lanes = slice(s * topk, (s + 1) * topk)
+            span_v[n, lines, :] = jnp.concatenate([all_values[t, r].astype(F32)[:, lanes] for r in range(team)], axis=1)
+
+    def densify(n, c, energy):
         tiles = []
         for s in range(fold):
-            lanes = slice(s * topk, (s + 1) * topk)
             lines = pl.ds(s * groups + c * SUBLANES, SUBLANES)
-            span_v[s] = jnp.concatenate([all_values[c, r].astype(F32)[:, lanes] for r in range(replicas)], axis=1)
-            tiles.append((span_a[lines, :], span_b[lines, :], span_v[s]))
-        for u in range(SUBLANES):
+            tiles.append([ref[n, lines, :] for ref in (span_a, span_b, span_v)])
+        for u, g in enumerate(members(c)):
             blocks = []
             for s in range(fold):
                 a, b, v = (tile[u:u + 1].astype(BF16) for tile in tiles[s])
                 row_hot = jnp.where(level == a, v, zero)
                 col_hot = jnp.where(level == b, one, zero)
-                blocks.append(dot_nt(row_hot, col_hot))
-            combined = jnp.concatenate(blocks, axis=1)
-            mixed[u] = combined.astype(BF16)
-            energy = energy + jnp.sum((combined * combined).reshape(BLOCK // SUBLANES, SUBLANES, width), axis=0)
+                block = dot_nt(row_hot, col_hot)
+                if n:
+                    block = block + partial[g * fold + s]
+                if n + 1 < teams:
+                    partial[g * fold + s] = block
+                blocks.append(block)
+            if n + 1 == teams:
+                combined = jnp.concatenate(blocks, axis=1)
+                mixed[g] = combined.astype(BF16)
+                energy = energy + jnp.sum((combined * combined).reshape(BLOCK // SUBLANES, SUBLANES, width), axis=0)
         return energy
 
     def decode(c):
-        mixed = mixes[c % 2]
-        tall_mix = jnp.concatenate([mixed[u] for u in range(SUBLANES)], axis=0)
-        across = dot(jnp.concatenate([tall_mix, tall_mix], axis=1), deep[...]).astype(BF16)
+        stack = jnp.concatenate([mixed[g] for g in members(c)], axis=0)
+        across = dot(jnp.concatenate([stack, stack], axis=1), deep[...]).astype(BF16)
         for u, g in enumerate(members(c)):
             block = across[u * BLOCK:(u + 1) * BLOCK]
             dense_ref[:, columns(g, width)] = dot(rows[...], jnp.concatenate([block, block], axis=0))
 
     energy = jnp.zeros((SUBLANES, width), F32)
-    for c in range(chunks):
-        each(lambda k: value_copy(c, k, source(k)).wait_recv())
-        energy = densify(c, energy)
-        if c:
-            decode(c - 1)
+    for n in range(teams):
+        t = lax.rem(home + n, teams)
+        count = team if n else team - 1
+        bulk(all_ids, id_sem, id_in, t, count).wait_recv()
+        name(n, t)
+        bulk(all_values, value_sem, value_in, t, count).wait_recv()
+        gather(n, t)
+        for c in range(chunks):
+            energy = densify(n, c, energy)
 
     energy = sum(energy[:, n * LANES:(n + 1) * LANES] for n in range(width // LANES))
     e_out[...] = energy
@@ -261,24 +278,16 @@
     def copy_tp(k, slot):
         return pltpu.make_async_remote_copy(
             src_ref=e_out, dst_ref=e_in.at[slot],
-            send_sem=e_send.at[k], recv_sem=e_recv.at[k],
-            device_id={"tensor": lax.rem(part + k, shards)}, device_id_type=MESH,
+            send_sem=e_send.at[k], recv_sem=e_recv.at[k], **mate(k),
         )
 
-    def start_tp(k, c):
-        copy_tp(k, part).start()
-        return c
-
-    def finish_tp(k, c):
-        copy_tp(k, lax.rem(part - k + shards, shards)).wait()
-        return c
-
-    lax.fori_loop(1, shards, start_tp, 0)
-    decode(chunks - 1)
-    each(lambda k: id_copy(k, me).wait_send())
+    each(1, shards, lambda k: copy_tp(k, part).start())
     for c in range(chunks):
-        each(lambda k: value_copy(c, k, me).wait_send())
-    lax.fori_loop(1, shards, finish_tp, 0)
+        decode(c)
+    for dst, sends, arrivals in ((all_ids, id_sem, id_in), (all_values, value_sem, value_in)):
+        for n in range(teams):
+            bulk(dst, sends, arrivals, n, team if n else team - 1).wait_send()
+    each(1, shards, lambda k: copy_tp(k, lax.rem(part - k + shards, shards)).wait())
 
 
 def finish(total, newm_ref, dense_ref, e_ref, newm_hbm, upd_hbm, upd, sems):
@@ -314,7 +323,10 @@
     fwd, inv = (jnp.asarray(np.concatenate([w, w], axis=0)) for w in both)
     deep = jnp.asarray(np.concatenate(np_halves(np.kron(np.eye(fold, dtype=np.float32), basis)), axis=0))
     rows = jnp.asarray(np.concatenate(np_halves(basis.T), axis=1))
-    depth = max(replicas * topk, LANES)
+    team = min(replicas, 2 * LANES // topk)
+    teams = replicas // team
+    depth = team * topk
+    assert teams * team == replicas and depth % LANES == 0
     vmem = pl.BlockSpec(memory_space=pltpu.VMEM)
     hbm = pl.BlockSpec(memory_space=pltpu.HBM)
     half = pltpu.VMEM((SUBLANES, height, width), BF16)
@@ -341,18 +353,23 @@
             half, half, half, half,
             pltpu.VMEM((height, groups * 2 * LANES), BF16),
             pltpu.VMEM((groups, LANES), jnp.int16),
-            pltpu.VMEM((replicas, groups, LANES), jnp.int16),
-            pltpu.VMEM((chunks, SUBLANES, LANES), BF16),
-            pltpu.VMEM((chunks, replicas, SUBLANES, LANES), BF16),
-            pltpu.VMEM((spans, depth), F32),
-            pltpu.VMEM((spans, depth), F32),
-            pltpu.VMEM((fold, SUBLANES, depth), F32),
-            half, half,
+            pltpu.VMEM((teams, team, groups, LANES), jnp.int16),
+            pltpu.VMEM((groups, LANES), F32),
+            pltpu.VMEM((groups, LANES), BF16),
+            pltpu.VMEM((teams, team, groups, LANES), BF16),
+            pltpu.VMEM((teams, spans, depth), F32),
+            pltpu.VMEM((teams, spans, depth), F32),
+            pltpu.VMEM((teams, spans, depth), F32),
+            pltpu.VMEM((spans, height, BLOCK), F32),
+            pltpu.VMEM((groups, height, width), BF16),
             pltpu.VMEM((SUBLANES, LANES), F32),
             pltpu.SemaphoreType.DMA((2, chunks)),
             pltpu.SemaphoreType.DMA((5,)),
-            pltpu.SemaphoreType.DMA((2, replicas)),
-            pltpu.SemaphoreType.DMA((chunks, 2, replicas)),
+            pltpu.SemaphoreType.DMA((1,)),
+            pltpu.SemaphoreType.DMA((1,)),
+            pltpu.SemaphoreType.DMA((teams,)),
+            pltpu.SemaphoreType.DMA((teams,)),
+            pltpu.SemaphoreType.REGULAR((replicas,)),
             pltpu.SemaphoreType.DMA((shards,)),
             pltpu.SemaphoreType.DMA((shards,)),
         ],

time: 23.2 us -> 19.1 us (0.82)
  the two profiles are of different devices: /device:TPU:0 before, /device:TPU:25 now
where the time goes in v2:
time: 19.1 us; the launch traced here: 19 us
  Pallas kernels  18.3 us (96%)
  between operations  0.64 us (3%)
    pallas_call x1, Pallas kernels, local(): pl.pallas_call(functools.partial(kernel, replicas, shards), out_shape=(ja...  17 us
    pallas_call x1, Pallas kernels, local(): pl.pallas_call(functools.partial(finish, float(height * cols * shards)),...  1.35 us

profile of v2, /device:TPU:25, one launch (start us, length us, event | category | flops | bytes accessed | tf_op | source)
XLA Modules:
  0.0 19.0 jit_solution(16394202245986529570)
XLA Ops:
  0.6 17.0 %demo_step.1 = (bf16[64,8192]{1,0:T(8,128)(2,1)S(1)}, f32[64,8192]{1,0:T(8,128)S(1)}, f32[2,8,128]{2,1,0:T(8,128)S(1)}) custom-call(bf16[64,8192]{1,0:T(8,128)(2,1)} %bitcast.6, bf16[64,8192]{1,0:T(8,128)(2,1)} %bitcast.7, s32[32,128]{1,0:T(8,128)} %bitcast.8, bf16[256,256]{1,0:T(8,128)(2,1)} %constant.8.clone.fwd_hbm, ...), custom_call_target="tpu_custom_call" | custom-call | tf_op jit(solution)/shard_map/demo_step/pallas_call | solution.py:334
  17.6 1.4 %finish.1 = (bf16[64,8192]{1,0:T(8,128)(2,1)}, bf16[64,8192]{1,0:T(8,128)(2,1)}) custom-call(bf16[64,8192]{1,0:T(8,128)(2,1)S(1)} %get-tuple-element.7.newm_ref, f32[64,8192]{1,0:T(8,128)S(1)} %get-tuple-element.8.dense_ref, f32[2,8,128]{2,1,0:T(8,128)S(1)} %get-tuple-element.9.e_ref), custom_call_target="tpu_custom_call" | custom-call | tf_op jit(solution)/shard_map/finish/pallas_call | solution.py:381

commit v3 on v2

--- a/solution.py
+++ b/solution.py
@@ -53,10 +53,17 @@
     return [jnp.concatenate(parts[2 * n:2 * n + 2], axis=1) for n in range(len(blocks))]
 
 
+def decode(blocks, deep, rows):
+    stack = jnp.concatenate(blocks, axis=0)
+    across = dot(jnp.concatenate([stack, stack], axis=1), deep).astype(BF16)
+    parts = [across[u * BLOCK:(u + 1) * BLOCK] for u in range(len(blocks))]
+    return [dot(rows, jnp.concatenate([part, part], axis=0)) for part in parts]
+
+
 def kernel(
     replicas, shards,
     grad_hbm, mom_hbm, idx_hbm, fwd_hbm, inv_hbm, deep_hbm, rows_hbm,
-    newm_ref, dense_ref, e_in,
+    newm_ref, dense_ref, e_in, last_ref, deep_ref, basis_ref,
     grad, mom, idx, fwd, inv, deep, rows,
     by_span, picks, high_even, low_even, high_odd, low_odd, factor,
     ids, all_ids, values, shipped, all_values, span_a, span_b, span_v, partial, mixed, e_out,
@@ -76,6 +83,8 @@
     teams = replicas // team
     depth = team * topk
     home = me // team
+    parts, half = shipped.shape[:2]
+    own = lax.rem(me, team)
 
     loads = [pltpu.make_async_copy(src, dst, c_sem.at[n]) for n, (src, dst) in enumerate(
         [(idx_hbm, idx), (fwd_hbm, fwd), (rows_hbm, rows), (inv_hbm, inv), (deep_hbm, deep)])]
@@ -167,31 +176,33 @@
         for g, block in zip(members(c), wide(spread, inv[...])):
             newm_ref[:, columns(g, width)] = (renew(g) - block).astype(BF16)
 
-    def copies(src, dst, sends, arrivals, j):
-        return pltpu.make_async_remote_copy(
-            src_ref=src, dst_ref=dst.at[home, lax.rem(me, team)],
-            send_sem=sends.at[0], recv_sem=arrivals.at[home], **peer(j),
-        )
+    def send(src, dst, send_sem, recv_sem, j):
+        pltpu.make_async_remote_copy(
+            src_ref=src, dst_ref=dst.at[home, own], send_sem=send_sem, recv_sem=recv_sem.at[home], **peer(j),
+        ).start()
 
     def send_ids(j):
-        copies(ids, all_ids, id_sem, id_in, j).start()
-
-    def send_values(j):
-        copies(shipped, all_values, value_sem, value_in, j).start()
+        send(ids, all_ids, id_sem.at[0], id_in, j)
+
+    def send_values(p, j):
+        send(shipped.at[p], all_values.at[p], value_sem.at[p], value_in.at[p], j)
+
+    def keep(src, dst, sem):
+        pltpu.make_async_copy(src, dst.at[home, own], sem.at[home]).start()
 
     def greet(j):
         pl.semaphore_wait(ready.at[j], 1)
         send_ids(j)
-        send_values(j)
-
-    def bulk(dst, sends, arrivals, t, count):
-        ref = dst.at[t, pl.ds(0, count)]
+        for p in range(parts):
+            send_values(p, j)
+
+    def bulk(ref, send_sem, recv_sem):
         return pltpu.make_async_remote_copy(
-            src_ref=ref, dst_ref=ref, send_sem=sends.at[0], recv_sem=arrivals.at[t], **peer(me),
+            src_ref=ref, dst_ref=ref, send_sem=send_sem, recv_sem=recv_sem, **peer(me),
         )
 
     each(0, me, send_ids)
-    all_ids[home, lax.rem(me, team)] = ids[...]
+    keep(ids, all_ids, id_in)
 
     loads[1].wait()
     for copy in slab(0):
@@ -204,17 +215,17 @@
                 copy.wait()
             transform(c + 1)
         pick(c)
-    shipped[...] = values[...].astype(BF16)
-    each(0, me, send_values)
-    all_values[home, lax.rem(me, team)] = shipped[...]
+        p = (c + 1) * SUBLANES // half - 1
+        if (c + 1) * SUBLANES == (p + 1) * half:
+            shipped[p] = values[pl.ds(p * half, half), :].astype(BF16)
+            each(0, me, functools.partial(send_values, p))
+            keep(shipped.at[p], all_values.at[p], value_in.at[p])
+    each(me + 1, replicas, greet)
 
     loads[3].wait()
-    restore(0)
-    each(me + 1, (home + 1) * team, greet)
-    for c in range(1, chunks):
+    loads[4].wait()
+    for c in range(chunks):
         restore(c)
-    each((home + 1) * team, replicas, greet)
-    loads[4].wait()
 
     def name(n, t):
         for s in range(fold):
@@ -224,11 +235,11 @@
             span_a[n, lines, :] = (named // BLOCK).astype(F32)
             span_b[n, lines, :] = (named % BLOCK).astype(F32)
 
-    def gather(n, t):
+    def gather(n, t, p):
         for s in range(fold):
-            lines = slice(s * groups, (s + 1) * groups)
+            lines = slice(s * groups + p * half, s * groups + (p + 1) * half)
             lanes = slice(s * topk, (s + 1) * topk)
-            span_v[n, lines, :] = jnp.concatenate([all_values[t, r].astype(F32)[:, lanes] for r in range(team)], axis=1)
+            span_v[n, lines, :] = jnp.concatenate([all_values[p, t, r].astype(F32)[:, lanes] for r in range(team)], axis=1)
 
     def densify(n, c, energy):
         tiles = []
@@ -253,23 +264,18 @@
                 energy = energy + jnp.sum((combined * combined).reshape(BLOCK // SUBLANES, SUBLANES, width), axis=0)
         return energy
 
-    def decode(c):
-        stack = jnp.concatenate([mixed[g] for g in members(c)], axis=0)
-        across = dot(jnp.concatenate([stack, stack], axis=1), deep[...]).astype(BF16)
-        for u, g in enumerate(members(c)):
-            block = across[u * BLOCK:(u + 1) * BLOCK]
-            dense_ref[:, columns(g, width)] = dot(rows[...], jnp.concatenate([block, block], axis=0))
-
     energy = jnp.zeros((SUBLANES, width), F32)
+    below = (home + teams - 1) // teams
+    first = home - below * (1 - 2 * own // team)
     for n in range(teams):
-        t = lax.rem(home + n, teams)
-        count = team if n else team - 1
-        bulk(all_ids, id_sem, id_in, t, count).wait_recv()
+        t = lax.rem(first + n, teams)
+        bulk(all_ids.at[t], id_sem.at[0], id_in.at[t]).wait_recv()
         name(n, t)
-        bulk(all_values, value_sem, value_in, t, count).wait_recv()
-        gather(n, t)
-        for c in range(chunks):
-            energy = densify(n, c, energy)
+        for p in range(parts):
+            bulk(all_values.at[p, t], value_sem.at[p], value_in.at[p, t]).wait_recv()
+            gather(n, t, p)
+            for c in range(p * half // SUBLANES, (p + 1) * half // SUBLANES):
+                energy = densify(n, c, energy)
 
     energy = sum(energy[:, n * LANES:(n + 1) * LANES] for n in range(width // LANES))
     e_out[...] = energy
@@ -282,26 +288,37 @@
         )
 
     each(1, shards, lambda k: copy_tp(k, part).start())
-    for c in range(chunks):
-        decode(c)
-    for dst, sends, arrivals in ((all_ids, id_sem, id_in), (all_values, value_sem, value_in)):
-        for n in range(teams):
-            bulk(dst, sends, arrivals, n, team if n else team - 1).wait_send()
+    for c in range(chunks - 1):
+        tiles = decode([mixed[g] for g in members(c)], deep[...], rows[...])
+        for g, tile in zip(members(c), tiles):
+            dense_ref[:, columns(g, width)] = tile
+    for u, g in enumerate(members(chunks - 1)):
+        last_ref[u] = mixed[g]
+    basis_ref[...] = rows[...]
+    deep_ref[...] = deep[...]
+    for n in range(teams):
+        slots = pl.ds(0, team if n else team - 1)
+        bulk(all_ids.at[n, slots], id_sem.at[0], id_in.at[n]).wait_send()
+        for p in range(parts):
+            bulk(all_values.at[p, n, slots], value_sem.at[p], value_in.at[p, n]).wait_send()
     each(1, shards, lambda k: copy_tp(k, lax.rem(part - k + shards, shards)).wait())
 
 
-def finish(total, newm_ref, dense_ref, e_ref, newm_hbm, upd_hbm, upd, sems):
-    first = pltpu.make_async_copy(newm_ref, newm_hbm, sems.at[0])
-    first.start()
+def finish(total, newm_ref, dense_ref, e_ref, last_ref, deep_ref, rows_ref, newm_hbm, upd_hbm, upd, sems):
     pieces = sems.shape[0] - 1
     stretch = upd.shape[1] // pieces
+    done = dense_ref.shape[1] // stretch
+    first = pltpu.make_async_copy(newm_ref, newm_hbm, sems.at[pieces])
+    first.start()
+    tiles = decode([last_ref[u] for u in range(last_ref.shape[0])], deep_ref[...], rows_ref[...])
     mean = jnp.sum(e_ref[...]) / total
     scale = lax.rsqrt(jnp.full((1, stretch), mean + EPSILON, F32))
     copies = []
     for n in range(pieces):
         cols = pl.ds(n * stretch, stretch)
-        upd[:, cols] = (dense_ref[:, cols] * scale).astype(BF16)
-        copies.append(pltpu.make_async_copy(upd.at[:, cols], upd_hbm.at[:, cols], sems.at[n + 1]))
+        block = dense_ref[:, cols] if n < done else jnp.concatenate(tiles, axis=1)
+        upd[:, cols] = (block * scale).astype(BF16)
+        copies.append(pltpu.make_async_copy(upd.at[:, cols], upd_hbm.at[:, cols], sems.at[n]))
         copies[-1].start()
     first.wait()
     for copy in copies:
@@ -325,21 +342,25 @@
     rows = jnp.asarray(np.concatenate(np_halves(basis.T), axis=1))
     team = min(replicas, 2 * LANES // topk)
     teams = replicas // team
+    parts = 1
     depth = team * topk
     assert teams * team == replicas and depth % LANES == 0
     vmem = pl.BlockSpec(memory_space=pltpu.VMEM)
     hbm = pl.BlockSpec(memory_space=pltpu.HBM)
     half = pltpu.VMEM((SUBLANES, height, width), BF16)
     operands = (gradient[0], momentum[0], indices.reshape(spans, topk).T, fwd, inv, deep, rows)
-    newm, dense, energy = pl.pallas_call(
+    newm, *rest = pl.pallas_call(
         functools.partial(kernel, replicas, shards),
         out_shape=(
             jax.ShapeDtypeStruct((height, cols), BF16),
-            jax.ShapeDtypeStruct((height, cols), F32),
+            jax.ShapeDtypeStruct((height, cols - SUBLANES * width), F32),
             jax.ShapeDtypeStruct((shards, SUBLANES, LANES), F32),
+            jax.ShapeDtypeStruct((SUBLANES, height, width), BF16),
+            jax.ShapeDtypeStruct(deep.shape, BF16),
+            jax.ShapeDtypeStruct(rows.shape, BF16),
         ),
         in_specs=[hbm] * 7,
-        out_specs=(vmem, vmem, vmem),
+        out_specs=(vmem,) * 6,
         scratch_shapes=[
             pltpu.VMEM((height, cols), BF16),
             pltpu.VMEM((height, cols), BF16),
@@ -355,8 +376,8 @@
             pltpu.VMEM((groups, LANES), jnp.int16),
             pltpu.VMEM((teams, team, groups, LANES), jnp.int16),
             pltpu.VMEM((groups, LANES), F32),
-            pltpu.VMEM((groups, LANES), BF16),
-            pltpu.VMEM((teams, team, groups, LANES), BF16),
+            pltpu.VMEM((parts, groups // parts, LANES), BF16),
+            pltpu.VMEM((parts, teams, team, groups // parts, LANES), BF16),
             pltpu.VMEM((teams, spans, depth), F32),
             pltpu.VMEM((teams, spans, depth), F32),
             pltpu.VMEM((teams, spans, depth), F32),
@@ -366,9 +387,9 @@
             pltpu.SemaphoreType.DMA((2, chunks)),
             pltpu.SemaphoreType.DMA((5,)),
             pltpu.SemaphoreType.DMA((1,)),
-            pltpu.SemaphoreType.DMA((1,)),
+            pltpu.SemaphoreType.DMA((parts,)),
             pltpu.SemaphoreType.DMA((teams,)),
-            pltpu.SemaphoreType.DMA((teams,)),
+            pltpu.SemaphoreType.DMA((parts, teams)),
             pltpu.SemaphoreType.REGULAR((replicas,)),
             pltpu.SemaphoreType.DMA((shards,)),
             pltpu.SemaphoreType.DMA((shards,)),
@@ -384,12 +405,12 @@
             jax.ShapeDtypeStruct((height, cols), BF16),
             jax.ShapeDtypeStruct((height, cols), BF16),
         ),
-        in_specs=[vmem] * 3,
+        in_specs=[vmem] * 6,
         out_specs=(hbm, hbm),
-        scratch_shapes=[pltpu.VMEM((height, cols), BF16), pltpu.SemaphoreType.DMA((5,))],
+        scratch_shapes=[pltpu.VMEM((height, cols), BF16), pltpu.SemaphoreType.DMA((chunks + 1,))],
         compiler_params=pltpu.CompilerParams(vmem_limit_bytes=8 * 2 ** 20),
         name="finish",
-    )(newm, dense, energy)
+    )(newm, *rest)
     return newm[None], update
 
 

time: 19.1 us -> 17.6 us (0.921)
  the two profiles are of different devices: /device:TPU:25 before, /device:TPU:0 now
where the time goes in v3:
time: 17.6 us; the launch traced here: 17.4 us
  Pallas kernels  16.8 us (95%)
  between operations  0.64 us (4%)
    pallas_call x1, Pallas kernels, local(): pl.pallas_call(functools.partial(kernel, replicas, shards), out_shape=(ja...  15.4 us
    pallas_call x1, Pallas kernels, local(): pl.pallas_call(functools.partial(finish, float(height * cols * shards)),...  1.36 us

profile of v3, /device:TPU:0, one launch (start us, length us, event | category | flops | bytes accessed | tf_op | source)
XLA Modules:
  0.0 17.4 jit_solution(500639673351225021)
XLA Ops:
  0.6 15.4 %demo_step.1 = (bf16[64,8192]{1,0:T(8,128)(2,1)S(1)}, f32[64,6144]{1,0:T(8,128)S(1)}, f32[2,8,128]{2,1,0:T(8,128)S(1)}, bf16[8,64,256]{2,1,0:T(8,128)(2,1)S(1)},...) custom-call(bf16[64,8192]{1,0:T(8,128)(2,1)} %bitcast.6, bf16[64,8192]{1,0:T(8,128)(2,1)} %bitcast.7, ...), custom_call_target="tpu_custom_call" | custom-call | tf_op jit(solution)/shard_map/demo_step/pallas_call | solution.py:352
  16.1 1.4 %finish.1 = (bf16[64,8192]{1,0:T(8,128)(2,1)}, bf16[64,8192]{1,0:T(8,128)(2,1)}) custom-call(bf16[64,8192]{1,0:T(8,128)(2,1)S(1)} %get-tuple-element.10.newm_ref, f32[64,6144]{1,0:T(8,128)S(1)} %get-tuple-element.11.dense_ref, f32[2,8,128]{2,1,0:T(8,128)S(1)} %get-tuple-element.12.e_ref, bf16[8,64,256]{2,1,0:T(8,128)(2,1)S(1)} %get-tuple-element.13.last_ref, ...), custom_call_target="tpu_custom_call" | custom-call | tf_op jit(solution)/shard_map/finish/pallas_call | solution.py:402

commit v4 on v3

--- a/solution.py
+++ b/solution.py
@@ -13,6 +13,7 @@
 SUBLANES = 8
 EPSILON = 1e-06
 DECAY = 0.999
+GAIN = 1.3725
 F32 = jnp.float32
 BF16 = jnp.bfloat16
 MESH = pl.DeviceIdType.MESH
@@ -55,7 +56,7 @@
 
 def decode(blocks, deep, rows):
     stack = jnp.concatenate(blocks, axis=0)
-    across = dot(jnp.concatenate([stack, stack], axis=1), deep).astype(BF16)
+    across = dot(stack, deep).astype(BF16)
     parts = [across[u * BLOCK:(u + 1) * BLOCK] for u in range(len(blocks))]
     return [dot(rows, jnp.concatenate([part, part], axis=0)) for part in parts]
 
@@ -67,7 +68,7 @@
     grad, mom, idx, fwd, inv, deep, rows,
     by_span, picks, high_even, low_even, high_odd, low_odd, factor,
     ids, all_ids, values, shipped, all_values, span_a, span_b, span_v, partial, mixed, e_out,
-    x_sem, c_sem, id_sem, value_sem, id_in, value_in, ready, e_send, e_recv,
+    x_sem, c_sem, id_sem, value_sem, id_in, twin_in, value_in, ready, e_send, e_recv,
 ):
     me = lax.axis_index("dp")
     part = lax.axis_index("tensor")
@@ -142,7 +143,7 @@
         return jnp.where(levels == picks[plane, pl.ds(g, 1), :].astype(BF16), one, zero)
 
     def columns(g, size):
-        return pl.ds(g * size, size)
+        return pl.ds(pl.multiple_of(g * size, size), size)
 
     def members(c):
         return range(c * SUBLANES, (c + 1) * SUBLANES)
@@ -170,10 +171,11 @@
 
     def restore(c):
         spread = []
-        for g in members(c):
+        batch = [c * SUBLANES + u for u in range(SUBLANES)]
+        for g in batch:
             col_hot = hot(tall, 1, g)
             spread.append(dot_nt(factor[:, columns(g, 2 * LANES)], jnp.concatenate([col_hot, col_hot], axis=1)))
-        for g, block in zip(members(c), wide(spread, inv[...])):
+        for g, block in zip(batch, wide(spread, inv[...])):
             newm_ref[:, columns(g, width)] = (renew(g) - block).astype(BF16)
 
     def send(src, dst, send_sem, recv_sem, j):
@@ -181,8 +183,23 @@
             src_ref=src, dst_ref=dst.at[home, own], send_sem=send_sem, recv_sem=recv_sem.at[home], **peer(j),
         ).start()
 
-    def send_ids(j):
-        send(ids, all_ids, id_sem.at[0], id_in, j)
+    def send_ids(arrivals, j):
+        send(ids, all_ids, id_sem.at[0], arrivals, j)
+
+    def twin(t):
+        return t * team + own
+
+    def forward(t):
+        src = all_ids.at[t, own]
+        bulk(src, id_sem.at[0], twin_in.at[t]).wait_recv()
+
+        def pass_on(j):
+            pltpu.make_async_remote_copy(
+                src_ref=src, dst_ref=src, send_sem=id_sem.at[0], recv_sem=id_in.at[t], **peer(j),
+            ).start()
+
+        each(home * team, me, pass_on)
+        each(me + 1, (home + 1) * team, pass_on)
 
     def send_values(p, j):
         send(shipped.at[p], all_values.at[p], value_sem.at[p], value_in.at[p], j)
@@ -192,16 +209,28 @@
 
     def greet(j):
         pl.semaphore_wait(ready.at[j], 1)
-        send_ids(j)
         for p in range(parts):
             send_values(p, j)
+
+    def greet_mate(j):
+        greet(j)
+        send_ids(id_in, j)
+
+    def greet_twin(t):
+        greet(twin(t))
+        send_ids(twin_in, twin(t))
+
+    def greet_others(t):
+        each(t * team, twin(t), greet)
+        each(twin(t) + 1, (t + 1) * team, greet)
 
     def bulk(ref, send_sem, recv_sem):
         return pltpu.make_async_remote_copy(
             src_ref=ref, dst_ref=ref, send_sem=send_sem, recv_sem=recv_sem, **peer(me),
         )
 
-    each(0, me, send_ids)
+    each(0, home, lambda t: send_ids(twin_in, twin(t)))
+    each(home * team, me, functools.partial(send_ids, id_in))
     keep(ids, all_ids, id_in)
 
     loads[1].wait()
@@ -220,12 +249,16 @@
             shipped[p] = values[pl.ds(p * half, half), :].astype(BF16)
             each(0, me, functools.partial(send_values, p))
             keep(shipped.at[p], all_values.at[p], value_in.at[p])
-    each(me + 1, replicas, greet)
-
+    each(home + 1, teams, greet_twin)
+    each(me + 1, (home + 1) * team, greet_mate)
     loads[3].wait()
     loads[4].wait()
-    for c in range(chunks):
-        restore(c)
+    early = chunks // (1 + me)
+    each(0, early, restore)
+    each(home + 1, teams, greet_others)
+    each(home + 1, teams, forward)
+    each(early, chunks, restore)
+    each(0, home, forward)
 
     def name(n, t):
         for s in range(fold):
@@ -252,24 +285,21 @@
                 a, b, v = (tile[u:u + 1].astype(BF16) for tile in tiles[s])
                 row_hot = jnp.where(level == a, v, zero)
                 col_hot = jnp.where(level == b, one, zero)
-                block = dot_nt(row_hot, col_hot)
-                if n:
-                    block = block + partial[g * fold + s]
-                if n + 1 < teams:
-                    partial[g * fold + s] = block
-                blocks.append(block)
-            if n + 1 == teams:
-                combined = jnp.concatenate(blocks, axis=1)
+                blocks.append(dot_nt(row_hot, col_hot))
+            combined = jnp.concatenate(blocks, axis=1)
+            if n:
+                combined = combined + partial[g]
+            if n + 1 < teams:
+                partial[g] = combined
+            else:
                 mixed[g] = combined.astype(BF16)
                 energy = energy + jnp.sum((combined * combined).reshape(BLOCK // SUBLANES, SUBLANES, width), axis=0)
         return energy
 
     energy = jnp.zeros((SUBLANES, width), F32)
-    below = (home + teams - 1) // teams
-    first = home - below * (1 - 2 * own // team)
     for n in range(teams):
-        t = lax.rem(first + n, teams)
-        bulk(all_ids.at[t], id_sem.at[0], id_in.at[t]).wait_recv()
+        t = lax.rem(home + n, teams)
+        bulk(all_ids.at[t, pl.ds(0, team - 1 if n else team)], id_sem.at[0], id_in.at[t]).wait_recv()
         name(n, t)
         for p in range(parts):
             bulk(all_values.at[p, t], value_sem.at[p], value_in.at[p, t]).wait_recv()
@@ -310,13 +340,16 @@
     done = dense_ref.shape[1] // stretch
     first = pltpu.make_async_copy(newm_ref, newm_hbm, sems.at[pieces])
     first.start()
-    tiles = decode([last_ref[u] for u in range(last_ref.shape[0])], deep_ref[...], rows_ref[...])
     mean = jnp.sum(e_ref[...]) / total
-    scale = lax.rsqrt(jnp.full((1, stretch), mean + EPSILON, F32))
+    scale = lax.rsqrt(jnp.full((1, stretch), mean + EPSILON, F32)) * (1.0 / GAIN)
     copies = []
     for n in range(pieces):
         cols = pl.ds(n * stretch, stretch)
-        block = dense_ref[:, cols] if n < done else jnp.concatenate(tiles, axis=1)
+        if n < done:
+            block = dense_ref[:, cols]
+        else:
+            blocks = [last_ref[u] for u in range(last_ref.shape[0])]
+            block = jnp.concatenate(decode(blocks, deep_ref[...], rows_ref[...]), axis=1)
         upd[:, cols] = (block * scale).astype(BF16)
         copies.append(pltpu.make_async_copy(upd.at[:, cols], upd_hbm.at[:, cols], sems.at[n]))
         copies[-1].start()
@@ -338,7 +371,7 @@
     pair = np.eye(2, dtype=np.float32)
     both = [np.concatenate(np_halves(np.kron(pair, w)), axis=1) for w in (basis.T, basis)]
     fwd, inv = (jnp.asarray(np.concatenate([w, w], axis=0)) for w in both)
-    deep = jnp.asarray(np.concatenate(np_halves(np.kron(np.eye(fold, dtype=np.float32), basis)), axis=0))
+    deep = jnp.asarray(np.kron(np.eye(fold, dtype=np.float32), GAIN * basis).astype(jnp.bfloat16))
     rows = jnp.asarray(np.concatenate(np_halves(basis.T), axis=1))
     team = min(replicas, 2 * LANES // topk)
     teams = replicas // team
@@ -381,13 +414,14 @@
             pltpu.VMEM((teams, spans, depth), F32),
             pltpu.VMEM((teams, spans, depth), F32),
             pltpu.VMEM((teams, spans, depth), F32),
-            pltpu.VMEM((spans, height, BLOCK), F32),
+            pltpu.VMEM((groups, height, width), F32),
             pltpu.VMEM((groups, height, width), BF16),
             pltpu.VMEM((SUBLANES, LANES), F32),
             pltpu.SemaphoreType.DMA((2, chunks)),
             pltpu.SemaphoreType.DMA((5,)),
             pltpu.SemaphoreType.DMA((1,)),
             pltpu.SemaphoreType.DMA((parts,)),
+            pltpu.SemaphoreType.DMA((teams,)),
             pltpu.SemaphoreType.DMA((teams,)),
             pltpu.SemaphoreType.DMA((parts, teams)),
             pltpu.SemaphoreType.REGULAR((replicas,)),

time: 17.6 us -> 17.1 us (0.972)
  Pallas kernels: 16.8 us -> 16.3 us
    pallas_call x1, Pallas kernels: 15.4 us -> 14.9 us  [local(): pl.pallas_call(functools.partial(kernel, replicas, shards), out_shape=(ja...]
where the time goes in v4:
time: 17.1 us; the launch traced here: 16.9 us
  Pallas kernels  16.3 us (95%)
  between operations  0.64 us (4%)
    pallas_call x1, Pallas kernels, local(): pl.pallas_call(functools.partial(kernel, replicas, shards), out_shape=(ja...  14.9 us
    pallas_call x1, Pallas kernels, local(): pl.pallas_call(functools.partial(finish, float(height * cols * shards)),...  1.36 us

profile of v4, /device:TPU:0, one launch (start us, length us, event | category | flops | bytes accessed | tf_op | source)
XLA Modules:
  0.0 16.9 jit_solution(11829354935754948011)
XLA Ops:
  0.6 14.9 %demo_step.1 = (bf16[64,8192]{1,0:T(8,128)(2,1)S(1)}, f32[64,6144]{1,0:T(8,128)S(1)}, f32[2,8,128]{2,1,0:T(8,128)S(1)}, bf16[8,64,256]{2,1,0:T(8,128)(2,1)S(1)},...) custom-call(bf16[64,8192]{1,0:T(8,128)(2,1)} %bitcast.6, bf16[64,8192]{1,0:T(8,128)(2,1)} %bitcast.7, ...), custom_call_target="tpu_custom_call" | custom-call | tf_op jit(solution)/shard_map/demo_step/pallas_call | solution.py:385
  15.5 1.4 %finish.1 = (bf16[64,8192]{1,0:T(8,128)(2,1)}, bf16[64,8192]{1,0:T(8,128)(2,1)}) custom-call(bf16[64,8192]{1,0:T(8,128)(2,1)S(1)} %get-tuple-element.10.newm_ref, f32[64,6144]{1,0:T(8,128)S(1)} %get-tuple-element.11.dense_ref, f32[2,8,128]{2,1,0:T(8,128)S(1)} %get-tuple-element.12.e_ref, bf16[8,64,256]{2,1,0:T(8,128)(2,1)S(1)} %get-tuple-element.13.last_ref, ...), custom_call_target="tpu_custom_call" | custom-call | tf_op jit(solution)/shard_map/finish/pallas_call | solution.py:436
